TPU v7x, 512 devices: a whole 4x4x16 slice. The times are simulated.
512 devices in a mesh: cuts: 4 (over z_hi), fsdp: 128 (over y, x, z_lo, core).
Axes of the slice: x: 4, y: 4, z: 16 (z_hi: 4, z_lo: 4; z = z_hi * 4 + z_lo), core: 2. Of those that a mesh axis runs over, the one named last changes fastest.
Arguments:
- tokens: bfloat16 [65536, 8192], P(('cuts', 'fsdp')), may hold values from -240 to 240
- norm_gain: bfloat16 [8192], P('fsdp'), may hold values from 0.5 to 1.5
- gate_weight: bfloat16 [8192, 256], P('fsdp'), may hold values from -0.0625 to 0.0625
- up_weight: bfloat16 [8192, 256], P('fsdp'), may hold values from -0.0625 to 0.0625
- down_weight: bfloat16 [256, 8192], P(None, 'fsdp'), may hold values from -0.375 to 0.375
- slice_grads: float32 [4, 3, 8192, 256], P('cuts', None, 'fsdp'), may hold values from -6 to 6
Outputs:
- branch_out: bfloat16 [65536, 8192], P(('cuts', 'fsdp'))
- grad_mean: float32 [3, 8192, 256], P(None, 'fsdp')
All inputs are finite; a program needn't handle non-finite values.
Results may differ from a plain program's by a relative error of at most 0.0065.
Values may be sent and summed in bfloat16 or wider, within the bound.
A program may use at most 64 MiB of HBM per device.

v0:
```python
import math

import jax
import jax.numpy as jnp
from jax import lax
from jax.sharding import Mesh
from jax.sharding import PartitionSpec as P

FSDP = ("fsdp_0", "fsdp_1", "fsdp_2", "fsdp_3")
CUTS_FSDP = ("cuts", "fsdp_0", "fsdp_1", "fsdp_2", "fsdp_3")


def from_everyone(shard, axis):
    copies = jnp.broadcast_to(shard, (lax.axis_size(axis), *shard.shape))
    return lax.all_to_all(copies, axis, split_axis=0, concat_axis=0, tiled=True)


def taken_together(shard, axis):
    everything = from_everyone(shard, axis)
    return jnp.sum(everything, axis=0)


def side_by_side(arrays, axis, dim, along):
    widths = [math.prod(a.shape[along:]) for a in arrays]
    both = jnp.concatenate(
        [a.reshape(*a.shape[:along], w) for a, w in zip(arrays, widths)], axis=along
    )
    filled = lax.all_gather(both, axis, axis=dim, tiled=True)
    tiles = jnp.split(filled, [sum(widths[:k]) for k in range(1, len(widths))], axis=along)
    return tuple(
        (b.reshape(*filled.shape[:along], *a.shape[along:]) for a, b in zip(arrays, tiles))
    )


def in_order(tiles, dim):
    tiles = jnp.moveaxis(tiles, 0, dim)
    shape = tiles.shape
    return tiles.reshape(*shape[:dim], shape[dim] * shape[dim + 1], *shape[dim + 2 :])


def gathered_by_axis(shard, axes, dim):
    far, near = axes
    leading = from_everyone(shard, far)
    tiles = jnp.swapaxes(from_everyone(leading, near), 0, 1)
    return in_order(tiles.reshape(-1, *shard.shape), dim)


def average_grads(slice_grads):
    summed = taken_together(slice_grads[0], "cuts")
    return summed / lax.axis_size("cuts")


def per_device(tokens, norm_gain, gate_weight, up_weight, down_weight, slice_grads):
    tok_float = tokens.astype(jnp.float32)
    inv_rms = lax.rsqrt(jnp.mean(tok_float * tok_float, axis=1, keepdims=True) + 1e-05)
    gathered = side_by_side((gate_weight, up_weight, norm_gain), FSDP, 0, 1)
    normed = (tok_float * inv_rms * gathered[2].astype(jnp.float32)[None, :]).astype(jnp.bfloat16)
    gate_out = jnp.dot(normed, gathered[0], preferred_element_type=jnp.float32)
    up_out = jnp.dot(normed, gathered[1], preferred_element_type=jnp.float32)
    hidden = (jax.nn.silu(gate_out) * up_out).astype(jnp.bfloat16)
    down_full = gathered_by_axis(down_weight, (("fsdp_0", "fsdp_1", "fsdp_2"), "fsdp_3"), 1)
    branch = jnp.dot(hidden, down_full, preferred_element_type=jnp.float32)
    grad_mean = average_grads(slice_grads)
    return (branch.astype(jnp.bfloat16), grad_mean)


def solution(mesh):
    finer = Mesh(
        mesh.devices.reshape(mesh.shape["cuts"], 4, 4, 4, 2),
        ("cuts", "fsdp_0", "fsdp_1", "fsdp_2", "fsdp_3"),
    )
    in_specs = (
        P(CUTS_FSDP, None),
        P(FSDP),
        P(FSDP, None),
        P(FSDP, None),
        P(None, FSDP),
        P("cuts", None, FSDP, None),
    )
    out_specs = (P(CUTS_FSDP, None), P(None, FSDP, None))
    return jax.shard_map(
        per_device, mesh=finer, in_specs=in_specs, out_specs=out_specs, check_vma=False
    )
```

profile of v0, /device:TPU:1, one launch (start us, length us, event | category | flops | bytes accessed | tf_op | source)
XLA Modules:
  0.0 277.5 jit_solution(340657969175162942)
XLA Ops:
  7.2 0.0 all-gather.2.cloned.1.call-start
  7.2 0.8 copy.13
  8.0 1.4 pad_maximum_fusion
  9.4 0.0 all-gather.2.cloned.1.call-update
  9.4 1.0 broadcast_in_dim.13
  10.4 50.1 %all_to_all.15 = f32[4,3,64,256]{3,2,1,0:T(8,128)S(1)} all-to-all(f32[4,3,64,256]{3,2,1,0:T(8,128)S(1)} %broadcast_in_dim.13), channel_id=1, replica_groups=mesh['cuts'=4,'fsdp_0'=4,'fsdp_1'=4,'fsdp_2'=4,'fsdp_3'=2] {'cuts'}, dimensions={0} | all-to-all | bytes 1572864 | tf_op jit(solution)/shard_map/all_to_all | solution.py:15
  60.5 2.3 broadcast_in_dim.11
  62.9 19.0 %all-to-all-start = ((bf16[64,256,64]{1,2,0:T(8,128)(2,1)}), bf16[64,256,64]{1,2,0:T(8,128)(2,1)S(1)}, u32[]{:S(2)}, u32[]{:S(2)}) async-start(bf16[64,256,64]{1,2,0:T(8,128)(2,1)} %broadcast_in_dim.11), calls=%async_computation | async-start | bytes 4194304 | tf_op jit(solution)/shard_map/all_to_all | solution.py:15
  81.9 2.1 fusion
  84.0 0.1 reduce_sum.19
  84.0 0.7 broadcast_multiply_fusion
  84.7 47.5 %all-to-all-done = bf16[64,256,64]{1,2,0:T(8,128)(2,1)S(1)} async-done(((bf16[64,256,64]{1,2,0:T(8,128)(2,1)}), bf16[64,256,64]{1,2,0:T(8,128)(2,1)S(1)}, u32[]{:S(2)}, u32[]{:S(2)}) %all-to-all-start) | async-done | bytes 2097184 | tf_op jit(solution)/shard_map/all_to_all | solution.py:15
  132.2 0.5 broadcast_in_dim.12
  132.7 9.3 %all_to_all.16 = bf16[2,64,256,64]{2,3,1,0:T(8,128)(2,1)S(1)} all-to-all(bf16[2,64,256,64]{2,3,1,0:T(8,128)(2,1)S(1)} %broadcast_in_dim.12), channel_id=1, replica_groups=mesh['cuts'=4,'fsdp_0'=4,'fsdp_1'=4,'fsdp_2'=4,'fsdp_3'=2] {'fsdp_3'}, dimensions={0} | all-to-all | bytes 8388608 | tf_op jit(solution)/shard_map/all_to_all | solution.py:15
  142.1 0.0 copy-start
  142.1 2.4 copy.14
  144.4 113.1 %all-gather.2.cloned.1.call-done = bf16[8192,513]{1,0:T(8,128)(2,1)} async-done(((bf16[64,513]{1,0:T(8,128)(2,1)}), bf16[8192,513]{1,0:T(8,128)(2,1)}) %all-gather.2.cloned.1.call-update) | async-done | bytes 8405008 | tf_op jit(solution)/shard_map/all_gather | solution.py:28
  257.6 2.2 convert_reduce_fusion
  259.8 0.0 copy-done
  259.8 3.0 %fusion.5 = f32[128,256]{1,0:T(8,128)S(1)} fusion(bf16[8192,513]{1,0:T(8,128)(2,1)} %all-gather.2.cloned.1.call-done, bf16[128,8192]{1,0:T(8,128)(2,1)S(1)} %copy-done, f32[8192]{0:T(1024)S(1)} %convert_reduce_fusion, f32[128]{0:T(128)S(1)} %add_rsqrt_fusion), kind=kOutput, calls=%fused_computation.8 | convolution fusion | flops 541065216 | bytes 6455808 | tf_op jit(solution)/shard_map/dot_general | solution.py:58
  262.8 7.9 %convolution_convert_fusion = bf16[128,8192]{1,0:T(8,128)(2,1)} fusion(bf16[256,8192]{0,1:T(8,128)(2,1)} %bitcast.10, bf16[8192,513]{1,0:T(8,128)(2,1)} %all-gather.2.cloned.1.call-done, bf16[128,8192]{1,0:T(8,128)(2,1)S(1)} %copy-done, f32[8192]{0:T(1024)S(1)} %convert_reduce_fusion, f32[128]{0:T(128)S(1)} %add_rsqrt_fusion, f32[128,256]{1,0:T(8,128)S(1)} %fusion.5), kind=kOutput, calls=%fused_computation | convolution fusion | flops 1079181312 | bytes 12747264 | tf_op jit(solution)/shard_map/dot_general | solution.py:62
  (1 shorter events, 0.0 us)
Async XLA Ops:
  7.2 250.4 %all-gather.2.cloned.1.call-start = ((), (), s32[]{:S(2)}) async-start(), calls=%async_computation.3 | async-start | bytes 10567680 | tf_op jit(solution)/shard_map/all_gather | solution.py:28
  62.9 69.4 %all-to-all-start = ((bf16[64,256,64]{1,2,0:T(8,128)(2,1)}), bf16[64,256,64]{1,2,0:T(8,128)(2,1)S(1)}, u32[]{:S(2)}, u32[]{:S(2)}) async-start(bf16[64,256,64]{1,2,0:T(8,128)(2,1)} %broadcast_in_dim.11), calls=%async_computation | async-start | bytes 4194304 | tf_op jit(solution)/shard_map/all_to_all | solution.py:15
  142.1 117.7 %copy-start = (bf16[128,8192]{1,0:T(8,128)(2,1)S(1)}, bf16[128,8192]{1,0:T(8,128)(2,1)}, u32[]{:S(2)}) copy-start(bf16[128,8192]{1,0:T(8,128)(2,1)} %param.6) | copy-start | bytes 6291460
Sparse Core Ops, SparseCore 0:
  10.1 247.3 all-gather.1
where the time goes:
time: 280 us; the launch traced here: 278 us
  waiting for transfers between devices  161 us (58%)
  blocking collectives  59.4 us (21%)
  starting transfers between devices  19 us (7%)
  between operations  14.1 us (5%)
  matrix products  10.9 us (4%)
  local copies, waits for them, and re-layouts  6.99 us (2%)
  other arithmetic  6.5 us (2%)
    all_gather x1, waiting for transfers between devices, side_by_side(): filled = lax.all_gather(both, axis, axis=dim, tiled=True)  113 us
    all_to_all x2, blocking collectives, from_everyone(): return lax.all_to_all(copies, axis, split_axis=0, concat_axis=0, tiled=True)  59.4 us
    all_to_all x1, waiting for transfers between devices, from_everyone(): return lax.all_to_all(copies, axis, split_axis=0, concat_axis=0, tiled=True)  47.5 us
    all_to_all x1, starting transfers between devices, from_everyone(): return lax.all_to_all(copies, axis, split_axis=0, concat_axis=0, tiled=True)  19 us
    dot_general x1, matrix products, per_device(): branch = jnp.dot(hidden, down_full, preferred_element_type=jnp.float32)  7.9 us
  transfers between devices with their start and end apart: 2, of which 2 were waited for; matrix products, arithmetic and copies ran while one was open for 3% of the time, Pallas kernels for 0%

commit v1 on v0

v1 whole, which is shorter than its diff:
```python
import jax
import jax.numpy as jnp
from jax import lax
from jax.experimental import pallas as pl
from jax.experimental.pallas import tpu as pltpu
from jax.sharding import Mesh
from jax.sharding import PartitionSpec as P

MESH = pl.DeviceIdType.MESH
FSDP = ("y", "x", "zl", "core")
CUTS_FSDP = ("cuts", "y", "x", "zl", "core")
ALL = slice(None)
NEAR = (0, -1, 1, 2)
F32 = jnp.float32
BF16 = jnp.bfloat16


class Numbers:
    def __init__(self):
        self.of = {}

    def __call__(self, *key):
        return self.of.setdefault(key, len(self.of))


def message_numbers():
    number = Numbers()
    for p in range(2):
        for d in range(2):
            number("t1", p, d)
            number("t4", p, d)
            number("z2", p, d)
            for j in NEAR:
                number("z1", p, d, j)
            for zr in NEAR:
                number("y2", p, d, zr)
                for j in NEAR:
                    number("y1", p, d, zr, j)
        for r in NEAR:
            for zr in NEAR:
                number("d2d", p, r, zr)
    for d in range(2):
        for name in ("rs1", "rs2", "ag1", "ag2"):
            number(name, d)
    return number


NUMBER = message_numbers()
N_MESSAGES = len(NUMBER.of)


def kernel(
    tok_hbm, gain_hbm, gate_hbm, up_hbm, down_hbm, grads_hbm,
    out, grad_out,
    buf_p, buf_q, tok, acc, hid, inv,
    gain_in, gate_in, up_in, down_in,
    grad_in, rs1, part, rs2,
    send_sem, recv_sem, in_sem,
):
    bufs = (buf_p, buf_q)
    h, y, x, zl, c = (lax.axis_index(a) for a in CUTS_FSDP)

    def ring(v, s, n=4):
        return lax.rem(v + (s + n), n)

    def neighbour(axis, s):
        if axis == "y":
            return {"y": ring(y, s)}
        if axis == "x":
            return {"x": ring(x, s)}
        if axis == "cut":
            return {"cuts": ring(h, s)}
        if axis == "core":
            return {"core": 1 - c}
        zz = lax.rem(h * 4 + zl + (s + 16), 16)
        return {"cuts": lax.div(zz, 4), "zl": lax.rem(zz, 4)}

    SIGN = (1, -1)
    BACK = (-1, 1)
    first = ("x", "y")
    last = ("y", "x")
    mine1 = (x, y)
    mine2 = (y, x)

    def shard(p, j, zr, r, half=None, core=None):
        i1 = ALL if j is ALL else ring(mine1[p], j)
        i2 = ring(mine2[p], r)
        yy, xx = (i2, i1) if p == 0 else (i1, i2)
        lanes = ALL if half is None else pl.ds(half * 128, 128)
        return bufs[p].at[yy, xx, ring(zl, zr), c if core is None else core, :, lanes]

    sent = []

    def copy_of(key, src, dst, axis, s):
        k = NUMBER.of[key]
        return pltpu.make_async_remote_copy(
            src_ref=src, dst_ref=dst, send_sem=send_sem.at[k], recv_sem=recv_sem.at[k],
            device_id=neighbour(axis, s), device_id_type=MESH,
        )

    def send(key, ref, axis, s, dst=None):
        copy = copy_of(key, ref, ref if dst is None else dst, axis, s)
        copy.start()
        sent.append(copy)

    def arrived(key, ref, axis, s):
        copy_of(key, ref, ref, axis, s).wait_recv()

    loads = [
        pltpu.make_async_copy(src, dst, in_sem.at[k])
        for k, (src, dst) in enumerate(
            (
                (gain_hbm, gain_in),
                (gate_hbm, gate_in),
                (down_hbm, down_in),
                (up_hbm, up_in),
                (grads_hbm.at[0], grad_in),
                (tok_hbm, tok),
            )
        )
    ]
    for load in loads:
        load.start()

    barrier = pltpu.get_barrier_semaphore()
    partners = [("cut", 1), ("cut", -1), ("x", 1), ("x", -1), ("y", 1), ("y", -1), ("z", 1), ("z", -1), ("core", 1)]
    for axis, s in partners:
        pl.semaphore_signal(barrier, inc=1, device_id=neighbour(axis, s), device_id_type=MESH)

    loads[0].wait()
    rows = lax.broadcasted_iota(jnp.int32, (64, 64), 0)
    cols = lax.broadcasted_iota(jnp.int32, (64, 64), 1)
    gain_row = jnp.broadcast_to(gain_in[...].astype(F32), (64, 64))
    gain = jnp.sum(jnp.where(rows == cols, gain_row, 0.0), axis=1, keepdims=True)
    loads[1].wait()
    buf_p[y, x, zl, c, 0:64, :] = (gate_in[...].astype(F32) * gain).astype(BF16)
    loads[2].wait()
    buf_p[y, x, zl, c, 64:96, :] = down_in[0:32]
    buf_q[y, x, zl, c, 64:96, :] = down_in[32:64]
    loads[3].wait()
    buf_q[y, x, zl, c, 0:64, :] = (up_in[...].astype(F32) * gain).astype(BF16)
    loads[4].wait()

    pl.semaphore_wait(barrier, len(partners))

    def quarter(ref, q, half=None):
        lanes = ALL if half is None else pl.ds(half * 128, 128)
        return ref.at[:, pl.ds(pl.multiple_of(q * 16, 16), 16), lanes]

    BOTH = [(p, d) for d in range(2) for p in range(2)]

    for p, d in BOTH:
        send(("t1", p, d), shard(p, 0, 0, 0), first[p], SIGN[d])
    for d in range(2):
        send(("rs1", d), quarter(grad_in, ring(h, 2), d), "cut", SIGN[d], rs1.at[d])
    for p, d in BOTH:
        send(("z1", p, d, 0), shard(p, 0, 0, 0), "z", SIGN[d])
    for p, d in BOTH:
        send(("y1", p, d, 0, 0), shard(p, 0, 0, 0), last[p], SIGN[d])

    loads[5].wait()

    def square(k, total):
        v = tok[:, pl.ds(pl.multiple_of(k * 128, 128), 128)].astype(F32)
        return total + v * v

    total = lax.fori_loop(0, 64, square, jnp.zeros((128, 128), F32), unroll=4)
    mean = jnp.sum(total, axis=1, keepdims=True) * (1.0 / 8192.0)
    inv[...] = jnp.broadcast_to(lax.rsqrt(mean + 1e-5), (128, 128))
    acc[...] = jnp.zeros_like(acc)

    for p, d in BOTH:
        j = BACK[d]
        arrived(("t1", p, d), shard(p, j, 0, 0), first[p], SIGN[d])
        send(("t4", p, d), shard(p, j, 0, 0, d), first[p], SIGN[d])
        for e in range(2):
            send(("z1", p, e, j), shard(p, j, 0, 0), "z", SIGN[e])
        for e in range(2):
            send(("y1", p, e, 0, j), shard(p, j, 0, 0), last[p], SIGN[e])
    for p, d in BOTH:
        zr = BACK[d]
        arrived(("z1", p, d, 0), shard(p, 0, zr, 0), "z", SIGN[d])
        for e in range(2):
            send(("y1", p, e, zr, 0), shard(p, 0, zr, 0), last[p], SIGN[e])
    for p in range(2):
        for d in range(2):
            arrived(("t4", p, d), shard(p, 2, 0, 0, d), first[p], SIGN[d])
        for e in range(2):
            send(("z1", p, e, 2), shard(p, 2, 0, 0), "z", SIGN[e])
        for e in range(2):
            send(("y1", p, e, 0, 2), shard(p, 2, 0, 0), last[p], SIGN[e])
        send(("d2d", p, 0, 0), shard(p, ALL, 0, 0), "core", 1)

    for d in range(2):
        arrived(("rs1", d), rs1.at[d], "cut", SIGN[d])
        q = pl.ds(pl.multiple_of(ring(h, SIGN[d]) * 16, 16), 16)
        part[d] = grad_in[:, q, :]
        lanes = pl.ds(d * 128, 128)
        part[d, :, :, lanes] = grad_in[:, q, lanes] + rs1[d]

    for j in (-1, 1):
        for p, d in BOTH:
            zr = BACK[d]
            arrived(("z1", p, d, j), shard(p, j, zr, 0), "z", SIGN[d])
            for e in range(2):
                send(("y1", p, e, zr, j), shard(p, j, zr, 0), last[p], SIGN[e])
        if j == -1:
            for d in range(2):
                send(("rs2", d), part.at[d], "cut", SIGN[d], rs2.at[d])
    for p, d in BOTH:
        zr = BACK[d]
        arrived(("z1", p, d, 2), shard(p, 2, zr, 0), "z", SIGN[d])
        send(("z2", p, d), shard(p, ALL, zr, 0, d), "z", SIGN[d])
        for e in range(2):
            send(("y1", p, e, zr, 2), shard(p, 2, zr, 0), last[p], SIGN[e])
        send(("d2d", p, 0, zr), shard(p, ALL, zr, 0), "core", 1)

    def last_axis(zr, js):
        for p, d in BOTH:
            r = BACK[d]
            for j in js:
                arrived(("y1", p, d, zr, 0 if j is ALL else j), shard(p, j, zr, r), last[p], SIGN[d])
            send(("y2", p, d, zr), shard(p, ALL, zr, r, d), last[p], SIGN[d])
            send(("d2d", p, r, zr), shard(p, ALL, zr, r), "core", 1)

    def far_plane(zr):
        for p in range(2):
            for d in range(2):
                arrived(("y2", p, d, zr), shard(p, ALL, zr, 2, d), last[p], SIGN[d])
            send(("d2d", p, 2, zr), shard(p, ALL, zr, 2), "core", 1)

    def multiply(r):
        for p in range(2):
            for zr in NEAR:
                arrived(("d2d", p, r, zr), shard(p, ALL, zr, r, core=1 - c), "core", 1)
            i2 = ring(mine2[p], r)
            n = pl.ds(p * 256, 256)

            def step(k, _, p=p, i2=i2, n=n):
                yy, xx = (i2, k) if p == 0 else (k, i2)
                w = bufs[p][yy, xx, :, :, 0:64, :].reshape(512, 256)
                t = tok[:, pl.ds(pl.multiple_of((yy * 4 + xx) * 512, 512), 512)]
                acc[:, n] += jnp.dot(t, w, preferred_element_type=F32)
                return 0

            lax.fori_loop(0, 4, step, 0)

    last_axis(0, NEAR)
    for p in range(2):
        for d in range(2):
            arrived(("z2", p, d), shard(p, ALL, 2, 0, d), "z", SIGN[d])
        for e in range(2):
            send(("y1", p, e, 2, 0), shard(p, ALL, 2, 0), last[p], SIGN[e])
        send(("d2d", p, 0, 2), shard(p, ALL, 2, 0), "core", 1)

    q = pl.ds(pl.multiple_of(h * 16, 16), 16)
    for d in range(2):
        arrived(("rs2", d), rs2.at[d], "cut", SIGN[d])
    grad_out[:, q, :] = (grad_in[:, q, :] + rs2[0] + rs2[1]) * 0.25

    last_axis(-1, NEAR)
    for d in range(2):
        send(("ag1", d), quarter(grad_out, h), "cut", SIGN[d])
    last_axis(1, NEAR)
    multiply(0)
    far_plane(0)
    last_axis(2, (ALL,))
    far_plane(-1)
    for d in range(2):
        arrived(("ag1", d), quarter(grad_out, ring(h, BACK[d])), "cut", SIGN[d])
        send(("ag2", d), quarter(grad_out, ring(h, BACK[d]), d), "cut", SIGN[d])
    multiply(-1)
    far_plane(1)
    multiply(1)
    far_plane(2)
    for d in range(2):
        arrived(("ag2", d), quarter(grad_out, ring(h, 2), d), "cut", SIGN[d])
    multiply(2)

    gate = acc[:, 0:256] * inv[:, 0:1]
    up = acc[:, 256:512] * inv[:, 0:1]
    hid[...] = (gate / (1.0 + jnp.exp(-gate)) * up).astype(BF16)

    def project(k, _):
        yy, xx = lax.div(k, 4), lax.rem(k, 4)
        w = jnp.concatenate([b[yy, xx, :, :, 64:96, :] for b in bufs], axis=2).reshape(512, 256)
        block = lax.dot_general(hid[...], w, (((1,), (1,)), ((), ())), preferred_element_type=F32)
        out[:, pl.ds(pl.multiple_of(k * 512, 512), 512)] = block.astype(BF16)
        return 0

    lax.fori_loop(0, 16, project, 0)

    for copy in sent:
        copy.wait_send()


def per_device(tokens, norm_gain, gate_weight, up_weight, down_weight, slice_grads):
    hbm = pl.BlockSpec(memory_space=pltpu.HBM)
    vmem = pl.BlockSpec(memory_space=pltpu.VMEM)
    return pl.pallas_call(
        kernel,
        out_shape=(
            jax.ShapeDtypeStruct(tokens.shape, BF16),
            jax.ShapeDtypeStruct(slice_grads.shape[1:], F32),
        ),
        in_specs=[hbm] * 6,
        out_specs=(vmem, vmem),
        scratch_shapes=[
            pltpu.VMEM((4, 4, 4, 2, 96, 256), BF16),
            pltpu.VMEM((4, 4, 4, 2, 96, 256), BF16),
            pltpu.VMEM((128, 8192), BF16),
            pltpu.VMEM((128, 512), F32),
            pltpu.VMEM((128, 256), BF16),
            pltpu.VMEM((128, 128), F32),
            pltpu.VMEM((1, 64), BF16),
            pltpu.VMEM((64, 256), BF16),
            pltpu.VMEM((64, 256), BF16),
            pltpu.VMEM((64, 256), BF16),
            pltpu.VMEM((3, 64, 256), F32),
            pltpu.VMEM((2, 3, 16, 128), F32),
            pltpu.VMEM((2, 3, 16, 256), F32),
            pltpu.VMEM((2, 3, 16, 256), F32),
            pltpu.SemaphoreType.DMA((N_MESSAGES,)),
            pltpu.SemaphoreType.DMA((N_MESSAGES,)),
            pltpu.SemaphoreType.DMA((6,)),
        ],
        compiler_params=pltpu.CompilerParams(
            collective_id=0, has_side_effects=True, vmem_limit_bytes=67043328
        ),
    )(tokens, norm_gain.reshape(1, 64), gate_weight, up_weight, down_weight.T, slice_grads)


def solution(mesh):
    finer = Mesh(mesh.devices.reshape(mesh.shape["cuts"], 4, 4, 4, 2), CUTS_FSDP)
    in_specs = (
        P(CUTS_FSDP, None),
        P(FSDP),
        P(FSDP, None),
        P(FSDP, None),
        P(None, FSDP),
        P("cuts", None, FSDP, None),
    )
    out_specs = (P(CUTS_FSDP, None), P(None, FSDP, None))
    return jax.shard_map(
        per_device, mesh=finer, in_specs=in_specs, out_specs=out_specs, check_vma=False
    )
```

time: 280 us -> 63.5 us (0.23)
  waiting for transfers between devices: 161 us -> 0 us
  blocking collectives: 59.4 us -> 0 us
  Pallas kernels: 0 us -> 58.9 us
  starting transfers between devices: 19 us -> 0 us
  between operations: 14.1 us -> 0.65 us
  matrix products: 10.9 us -> 0 us
  other arithmetic: 6.5 us -> 0 us
  local copies, waits for them, and re-layouts: 6.99 us -> 3.82 us
    all_gather x1 -> x0, waiting for transfers between devices: 113 us -> none  [side_by_side(): filled = lax.all_gather(both, axis, axis=dim, tiled=True)]
    all_to_all x2 -> x0, blocking collectives: 59.4 us -> none  [from_everyone(): return lax.all_to_all(copies, axis, split_axis=0, concat_axis=0, tiled=True)]
    pallas_call x0 -> x1, Pallas kernels: none -> 58.9 us  [per_device(): pl.pallas_call(kernel, out_shape=(jax.ShapeDtypeStruct(tokens.shape, BF16...]
    all_to_all x1 -> x0, waiting for transfers between devices: 47.5 us -> none  [from_everyone(): return lax.all_to_all(copies, axis, split_axis=0, concat_axis=0, tiled=True)]
    all_to_all x1 -> x0, starting transfers between devices: 19 us -> none  [from_everyone(): return lax.all_to_all(copies, axis, split_axis=0, concat_axis=0, tiled=True)]
    dot_general x2 -> x0, matrix products: 10.9 us -> none  [the longest x1 7.9 us: per_device(): branch = jnp.dot(hidden, down_full, preferred_element_type=jnp.float32)]
    broadcast_in_dim x3 -> x0, local copies, waits for them, and re-layouts: 3.84 us -> none  [from_everyone(): copies = jnp.broadcast_to(shard, (lax.axis_size(axis), *shard.shape))]
    unnamed x2 -> x4, local copies, waits for them, and re-layouts: 0.01 us -> 3.82 us
  transfers between devices with their start and end apart: 2 -> 0, of which waited for: 2 -> 0; matrix products, arithmetic and copies ran while one was open for 3% -> 0% of each run, Pallas kernels for 0% -> 0%
where the time goes in v1:
time: 63.5 us; the launch traced here: 63.4 us
  Pallas kernels  58.9 us (93%)
  local copies, waits for them, and re-layouts  3.82 us (6%)
  between operations  0.65 us (1%)
    pallas_call x1, Pallas kernels, per_device(): pl.pallas_call(kernel, out_shape=(jax.ShapeDtypeStruct(tokens.shape, BF16...  58.9 us
    unnamed x4, local copies, waits for them, and re-layouts  3.82 us

profile of v1, /device:TPU:1, one launch (start us, length us, event | category | flops | bytes accessed | tf_op | source)
XLA Modules:
  0.0 63.4 jit_solution(7262797401447990258)
XLA Ops:
  0.6 58.9 %shard_map.77 = (bf16[128,8192]{1,0:T(8,128)(2,1)}, f32[3,64,256]{2,1,0:T(8,128)}) custom-call(bf16[128,8192]{1,0:T(8,128)(2,1)} %tok_hbm.1, bf16[1,64]{1,0:T(2,128)(2,1)} %bitcast.3, bf16[64,256]{1,0:T(8,128)(2,1)} %gate_hbm.1, bf16[64,256]{1,0:T(8,128)(2,1)} %up_hbm.1, bf16[64,256]{1,0:T(8,128)(2,1)} %bitcast.2, f32[1,3,64,256]{3,2,1,0:T(8,128)} %grads_hbm.1), custom_call_target="tpu_custom_call" | custom-call | tf_op jit(solution)/shard_map/pallas_call | solution.py:300
  59.5 0.0 copy-start
  59.6 3.1 %copy.10 = bf16[128,8192]{1,0:T(8,128)(2,1)} copy(bf16[128,8192]{1,0:T(8,128)(2,1)} %get-tuple-element.4) | data formatting | bytes 4194304
  62.7 0.0 copy-done
  62.7 0.7 %copy.11 = f32[3,64,256]{2,1,0:T(8,128)} copy(f32[3,64,256]{2,1,0:T(8,128)S(1)} %copy-done) | data formatting | bytes 393216
Async XLA Ops:
  59.5 3.1 %copy-start = (f32[3,64,256]{2,1,0:T(8,128)S(1)}, f32[3,64,256]{2,1,0:T(8,128)}, u32[]{:S(2)}) copy-start(f32[3,64,256]{2,1,0:T(8,128)} %get-tuple-element.5) | copy-start | bytes 589828

commit v2 on v1

v2 whole, which is shorter than its diff:
```python
import jax
import jax.numpy as jnp
from jax import lax
from jax.experimental import pallas as pl
from jax.experimental.pallas import tpu as pltpu
from jax.sharding import Mesh
from jax.sharding import PartitionSpec as P

MESH = pl.DeviceIdType.MESH
FSDP = ("y", "x", "zl", "core")
CUTS_FSDP = ("cuts", "y", "x", "zl", "core")
ALL = slice(None)
NEAR = (0, -1, 1, 2)
F32 = jnp.float32
BF16 = jnp.bfloat16


PARTS = range(2)
WAYS = range(2)

RECV = [("t1", p, d) for p in PARTS for d in WAYS]
RECV += [("t4", p) for p in PARTS] + [("z2", p) for p in PARTS] + [("c0", p) for p in PARTS]
RECV += [("z1", p, d, j) for p in PARTS for d in WAYS for j in NEAR]
RECV += [("g1", p, d, zr) for p in PARTS for d in WAYS for zr in NEAR]
RECV += [("g2", p, zr) for p in PARTS for zr in NEAR]
RECV += [("d1", p, d, zr) for p in PARTS for d in WAYS for zr in NEAR[1:]]
RECV += [("d2", p, zr) for p in PARTS for zr in NEAR[1:]]
RECV += [(name, p, r) for name in ("cg", "cd") for p in PARTS for r in (-1, 1, 2)]
GRADS = [(name, d) for name in ("rs1", "rs2", "ag1", "ag2") for d in WAYS]
RECV = {key: k for k, key in enumerate(RECV + GRADS)}
KINDS = ("t1", "t4", "z1", "z2", "g1", "g2", "d1", "d2", "c0", "cg", "cd")
SENT = {key: k for k, key in enumerate([(kind, p) for kind in KINDS for p in PARTS] + GRADS)}


def kernel(
    tok_hbm, gain_hbm, gate_hbm, up_hbm, down_hbm, grads_hbm,
    out, grad_out,
    buf_p, buf_q, tok, acc, hid, inv,
    gain_in, gate_in, up_in, down_in,
    grad_in, rs1, part, rs2, mean_out,
    send_sem, recv_sem, in_sem, here,
):
    bufs = (buf_p, buf_q)
    h, y, x, zl, c = (lax.axis_index(a) for a in CUTS_FSDP)

    def ring(v, s, n=4):
        return lax.rem(v + (s + n), n)

    def neighbour(axis, s):
        if axis == "y":
            return {"y": ring(y, s)}
        if axis == "x":
            return {"x": ring(x, s)}
        if axis == "cut":
            return {"cuts": ring(h, s)}
        if axis == "core":
            return {"core": 1 - c}
        zz = lax.rem(h * 4 + zl + (s + 16), 16)
        return {"cuts": lax.div(zz, 4), "zl": lax.rem(zz, 4)}

    SIGN = (1, -1)
    BACK = (-1, 1)
    first = ("x", "y")
    last = ("y", "x")
    mine1 = (x, y)
    mine2 = (y, x)

    GATED, DOWN = pl.ds(0, 64), pl.ds(64, 32)

    def shard(p, j, zr, r, half=None, rows=ALL, core=None):
        i1 = ALL if j is ALL else ring(mine1[p], j)
        iz = ALL if zr is ALL else ring(zl, zr)
        i2 = ring(mine2[p], r)
        yy, xx = (i2, i1) if p == 0 else (i1, i2)
        lanes = ALL if half is None else pl.ds(half * 128, 128)
        return bufs[p].at[yy, xx, iz, c if core is None else core, rows, lanes]

    def copy_of(key, src, dst, axis, s):
        return pltpu.make_async_remote_copy(
            src_ref=src,
            dst_ref=dst,
            send_sem=send_sem.at[SENT[key if key in GRADS else key[:2]]],
            recv_sem=recv_sem.at[RECV[key]],
            device_id=neighbour(axis, s),
            device_id_type=MESH,
        )

    def give(key, axis, s, *where, **also):
        ref = shard(*where, **also)
        copy_of(key, ref, ref, axis, s).start()

    def arrived(key, ref):
        copy_of(key, ref, ref, "core", 1).wait_recv()

    def taken(key, *where, **also):
        arrived(key, shard(*where, **also))

    def all_sent():
        for p in PARTS:
            b = bufs[p]
            for kind, ref in (
                ("t1", b.at[0, 0, 0]),
                ("t4", b.at[0, 0, 0, 0]),
                ("z1", b.at[0, 0]),
                ("g1", b.at[0, 0:3]),
                ("g2", b.at[0, 0:3, 0:2]),
                ("d1", b.at[0, 0]),
                ("d2", b.at[0, 0, 0:2]),
                ("c0", b.at[0, 0:2]),
                ("cg", b.at[0:3, 0:2, :, :, 0:64]),
                ("cd", b.at[0:3, 0:2, :, :, 64:96]),
            ):
                pltpu.make_async_remote_copy(
                    src_ref=ref,
                    dst_ref=ref,
                    send_sem=send_sem.at[SENT[kind, p]],
                    recv_sem=recv_sem.at[0],
                    device_id=neighbour("core", 1),
                    device_id_type=MESH,
                ).wait_send()

            def second(ref):
                copy_of(("z2", p), ref, ref, "core", 1).wait_send()

            @pl.when(jnp.logical_or(zg == 0, zg == 15))
            def _():
                second(b.at[0, 0, 0])

            @pl.when(jnp.logical_or(zg == 1, zg == 2))
            def _():
                second(b.at[0, 0:3, 0])

            @pl.when(jnp.logical_and(zg > 2, zg < 15))
            def _():
                second(b.at[0, 0, 0:2])

        for d in WAYS:
            for name, ref in (("rs1", rs1.at[d]), ("rs2", rs2.at[d]), ("ag1", mean_out.at[0]), ("ag2", mean_out.at[0, :, :, 0:128])):
                copy_of((name, d), ref, ref, "core", 1).wait_send()

    def tell(k, s):
        pl.semaphore_signal(here.at[k], inc=1, device_id=neighbour("z", s), device_id_type=MESH)

    def told(k):
        pl.semaphore_wait(here.at[k], 1)

    zg = h * 4 + zl

    loads = [
        pltpu.make_async_copy(src, dst, in_sem.at[k])
        for k, (src, dst) in enumerate(
            (
                (gain_hbm, gain_in),
                (gate_hbm, gate_in),
                (down_hbm, down_in),
                (up_hbm, up_in),
                (grads_hbm.at[0], grad_in),
                (tok_hbm, tok),
            )
        )
    ]
    for load in loads:
        load.start()

    barrier = pltpu.get_barrier_semaphore()
    partners = [("x", 1), ("x", -1), ("y", 1), ("y", -1), ("z", -1), ("core", 1)]
    for axis, s in partners:
        pl.semaphore_signal(barrier, inc=1, device_id=neighbour(axis, s), device_id_type=MESH)

    loads[0].wait()
    rows = lax.broadcasted_iota(jnp.int32, (64, 64), 0)
    cols = lax.broadcasted_iota(jnp.int32, (64, 64), 1)
    gain_row = jnp.broadcast_to(gain_in[...].astype(F32), (64, 64))
    gain = jnp.sum(jnp.where(rows == cols, gain_row, 0.0), axis=1, keepdims=True)
    loads[1].wait()
    buf_p[y, x, zl, c, 0:64, :] = (gate_in[...].astype(F32) * gain).astype(BF16)
    loads[2].wait()
    buf_p[y, x, zl, c, 64:96, :] = down_in[0:32]
    buf_q[y, x, zl, c, 64:96, :] = down_in[32:64]
    loads[3].wait()
    buf_q[y, x, zl, c, 0:64, :] = (up_in[...].astype(F32) * gain).astype(BF16)

    pl.semaphore_wait(barrier, len(partners))

    def quarter(ref, q, half=None):
        lanes = ALL if half is None else pl.ds(half * 128, 128)
        return ref.at[:, pl.ds(pl.multiple_of(q * 16, 16), 16), lanes]

    BOTH = [(p, d) for d in WAYS for p in PARTS]

    def along_z(p, j):
        give(("z1", p, 0, j), "z", 1, p, j, 0, 0)

        @pl.when(zg > 0)
        def _():
            give(("z1", p, 1, j), "z", -1, p, j, 0, 0)

    def along_last(p, zr, j):
        for e in WAYS:
            give(("g1", p, e, zr), last[p], SIGN[e], p, j, zr, 0, rows=ALL if zr == 0 else GATED)

    for p, d in BOTH:
        give(("t1", p, d), first[p], SIGN[d], p, 0, 0, 0)
    tell(0, 1)
    for p in PARTS:
        give(("z1", p, 0, 0), "z", 1, p, 0, 0, 0)
    for p in PARTS:
        along_last(p, 0, 0)

    def below():
        told(0)
        tell(1, -1)
        tell(2, 1)

    def four_away():
        tell(3, -2)
        tell(4, 2)

    def exchange(d):
        src = quarter(grad_in, ring(h, 2), d)
        copy_of(("rs1", d), src, rs1.at[d], "cut", SIGN[d]).start()

    @pl.when(zg > 0)
    def _():
        below()
        for p in PARTS:
            give(("z1", p, 1, 0), "z", -1, p, 0, 0, 0)

    loads[4].wait()
    loads[5].wait()

    def square(k, total):
        v = tok[:, pl.ds(pl.multiple_of(k * 128, 128), 128)].astype(F32)
        return total + v * v

    total = lax.fori_loop(0, 64, square, jnp.zeros((128, 128), F32), unroll=4)
    mean = jnp.sum(total, axis=1, keepdims=True) * (1.0 / 8192.0)
    inv[...] = jnp.broadcast_to(lax.rsqrt(mean + 1e-5), (128, 128))
    acc[...] = jnp.zeros_like(acc)

    @pl.when(zg < 15)
    def _():
        told(1)

    @pl.when(zg > 1)
    def _():
        told(2)

    @pl.when(jnp.logical_and(zg > 1, zg < 15))
    def _():
        four_away()

    @pl.when(zg == 15)
    def _():
        told(1)
        four_away()

    @pl.when(zg < 13)
    def _():
        told(3)
        exchange(0)

    @pl.when(zg > 3)
    def _():
        told(4)
        exchange(1)

    def first_axis(p, d):
        j = BACK[d]
        taken(("t1", p, d), p, j, 0, 0)
        give(("t4", p), first[p], SIGN[d], p, j, 0, 0, half=d)
        along_z(p, j)
        along_last(p, 0, j)

    for p, d in BOTH:
        first_axis(p, d)

    def onward(p, d, j, half=True):
        give(("z2", p), "z", SIGN[d], p, j, BACK[d], 0, half=d if half else None)

    def from_z(d, js):
        zr = BACK[d]
        for j in js:
            for p in PARTS:
                taken(("z1", p, d, j), p, j, zr, 0)
                if d == 0:

                    @pl.when(jnp.logical_and(zg > 0, zg < 15))
                    def _():
                        onward(p, d, j)

                else:

                    @pl.when(zg > 2)
                    def _():
                        onward(p, d, j)

                    @pl.when(jnp.logical_or(zg == 1, zg == 2))
                    def _():
                        onward(p, d, j, half=False)

                along_last(p, zr, j)
        if js[-1] == 2:
            for p in PARTS:
                give(("c0", p), "core", 1, p, ALL, zr, 0)

    def first_far(p):
        taken(("t4", p), p, 2, 0, 0)
        along_z(p, 2)
        along_last(p, 0, 2)
        give(("c0", p), "core", 1, p, ALL, 0, 0)

    def down_near(zr):
        for p, d in BOTH:
            give(("d1", p, d, zr), last[p], SIGN[d], p, ALL, zr, 0, rows=DOWN)

    def gated_near(zr):
        for p, d in BOTH:
            r = BACK[d]
            rows = ALL if zr == 0 else GATED
            taken(("g1", p, d, zr), p, ALL, zr, r, rows=rows)
            give(("g2", p, zr), last[p], SIGN[d], p, ALL, zr, r, half=d, rows=rows)
            give(("cg", p, r), "core", 1, p, ALL, zr, r, rows=GATED)
            if zr == 0:
                give(("cd", p, r), "core", 1, p, ALL, zr, r, rows=DOWN)

    def gated_far(zr):
        for p in PARTS:
            taken(("g2", p, zr), p, ALL, zr, 2, rows=ALL if zr == 0 else GATED)
            give(("cg", p, 2), "core", 1, p, ALL, zr, 2, rows=GATED)
            if zr == 0:
                give(("cd", p, 2), "core", 1, p, ALL, zr, 2, rows=DOWN)

    def down_next(zr):
        for p, d in BOTH:
            r = BACK[d]
            taken(("d1", p, d, zr), p, ALL, zr, r, rows=DOWN)
            give(("d2", p, zr), last[p], SIGN[d], p, ALL, zr, r, half=d, rows=DOWN)
            give(("cd", p, r), "core", 1, p, ALL, zr, r, rows=DOWN)

    def down_far(zr):
        for p in PARTS:
            taken(("d2", p, zr), p, ALL, zr, 2, rows=DOWN)
            give(("cd", p, 2), "core", 1, p, ALL, zr, 2, rows=DOWN)

    def across_z():
        for p in PARTS:
            taken(("z2", p), p, ALL, 2, 0)
            along_last(p, 2, ALL)
            give(("c0", p), "core", 1, p, ALL, 2, 0)

    def multiply(r):
        for p in PARTS:
            if r == 0:
                taken(("c0", p), p, ALL, ALL, 0, core=1 - c)
            else:
                taken(("cg", p, r), p, ALL, ALL, r, rows=GATED, core=1 - c)
            i2 = ring(mine2[p], r)
            n = pl.ds(p * 256, 256)
            total = acc[:, n]
            for k in range(4):
                yy, xx = (i2, k) if p == 0 else (k, i2)
                w = bufs[p][yy, xx, :, :, 0:64, :].reshape(512, 256)
                t = tok[:, pl.ds(pl.multiple_of((yy * 4 + xx) * 512, 512), 512)]
                total = total + jnp.dot(t, w, preferred_element_type=F32)
            acc[:, n] = total

    def grads_partial():
        for d in WAYS:
            arrived(("rs1", d), rs1.at[d])
            q = pl.ds(pl.multiple_of(ring(h, SIGN[d]) * 16, 16), 16)
            part[d] = grad_in[:, q, :]
            lanes = pl.ds(d * 128, 128)
            part[d, :, :, lanes] = grad_in[:, q, lanes] + rs1[d]

    def grads_send():
        for d in WAYS:
            copy_of(("rs2", d), part.at[d], rs2.at[d], "cut", SIGN[d]).start()

    def grads_own():
        q = pl.ds(pl.multiple_of(h * 16, 16), 16)
        for d in WAYS:
            arrived(("rs2", d), rs2.at[d])
        mean_out[h] = ((grad_in[:, q, :] + rs2[0] + rs2[1]) * 0.25).astype(BF16)

    def grads_give():
        for d in WAYS:
            copy_of(("ag1", d), mean_out.at[h], mean_out.at[h], "cut", SIGN[d]).start()

    def grads_next():
        for d in WAYS:
            arrived(("ag1", d), mean_out.at[ring(h, BACK[d])])
            half = mean_out.at[ring(h, BACK[d]), :, :, pl.ds(d * 128, 128)]
            copy_of(("ag2", d), half, half, "cut", SIGN[d]).start()

    first_far(0)
    first_far(1)
    from_z(1, (0,))

    @pl.when(zg > 0)
    def _():
        from_z(0, (0,))

    @pl.when(zg == 0)
    def _():
        below()
        for p in PARTS:
            for j in NEAR:
                give(("z1", p, 1, j), "z", -1, p, j, 0, 0)
            onward(p, 1, 0)

    @pl.when(zg < 2)
    def _():
        told(2)
        four_away()

    gated_near(0)
    from_z(1, (-1, 1, 2))

    @pl.when(zg == 0)
    def _():
        for p in PARTS:
            for j in NEAR[1:]:
                onward(p, 1, j)

    down_near(1)

    @pl.when(zg > 12)
    def _():
        told(3)
        exchange(0)

    @pl.when(zg < 4)
    def _():
        told(4)
        exchange(1)

    grads_partial()
    grads_send()

    @pl.when(zg < 2)
    def _():
        gated_near(1)
        down_next(1)

    @pl.when(zg == 0)
    def _():
        from_z(0, (0,))

    from_z(0, (-1, 1, 2))
    down_near(-1)

    @pl.when(zg > 1)
    def _():
        gated_near(1)
        down_next(1)

    gated_near(-1)
    across_z()
    down_near(2)
    down_next(-1)
    grads_own()
    grads_give()
    gated_near(2)
    grads_next()
    down_next(2)
    gated_far(0)
    gated_far(1)
    multiply(0)
    gated_far(-1)
    multiply(-1)
    gated_far(2)
    multiply(1)
    down_far(1)
    down_far(-1)
    multiply(2)

    gate = acc[:, 0:256] * inv[:, 0:1]
    up = acc[:, 256:512] * inv[:, 0:1]
    hid[...] = (gate / (1.0 + jnp.exp(-gate)) * up).astype(BF16)

    def project(yy, xx):
        w = jnp.concatenate([b[yy, xx, :, :, 64:96, :] for b in bufs], axis=2).reshape(512, 256)
        block = lax.dot_general(hid[...], w, (((1,), (1,)), ((), ())), preferred_element_type=F32)
        out[:, pl.ds(pl.multiple_of((yy * 4 + xx) * 512, 512), 512)] = block.astype(BF16)

    for p in PARTS:
        for r in (-1, 1):
            taken(("cd", p, r), p, ALL, ALL, r, rows=DOWN, core=1 - c)

    def near(k, _):
        for i in range(3):
            project(ring(y, k - 1), ring(x, i - 1))
        return 0

    def last_part():
        for p in PARTS:
            taken(("cd", p, 2), p, ALL, ALL, 2, rows=DOWN, core=1 - c)
        for k in range(4):
            project(ring(y, 2), k)
        for k in range(3):
            project(ring(y, k - 1), ring(x, 2))

    def finish():
        for d in WAYS:
            arrived(("ag2", d), mean_out.at[ring(h, 2), :, :, pl.ds(d * 128, 128)])
        for k in range(4):
            grad_out[:, k * 16 : k * 16 + 16, :] = mean_out[k].astype(F32)

    down_far(2)
    lax.fori_loop(0, 3, near, 0)
    finish()
    last_part()
    all_sent()


def per_device(tokens, norm_gain, gate_weight, up_weight, down_weight, slice_grads):
    hbm = pl.BlockSpec(memory_space=pltpu.HBM)
    vmem = pl.BlockSpec(memory_space=pltpu.VMEM)
    return pl.pallas_call(
        kernel,
        out_shape=(
            pltpu.VMEM(tokens.shape, BF16),
            pltpu.VMEM(slice_grads.shape[1:], F32),
        ),
        in_specs=[hbm] * 6,
        out_specs=(vmem, vmem),
        scratch_shapes=[
            pltpu.VMEM((4, 4, 4, 2, 96, 256), BF16),
            pltpu.VMEM((4, 4, 4, 2, 96, 256), BF16),
            pltpu.VMEM((128, 8192), BF16),
            pltpu.VMEM((128, 512), F32),
            pltpu.VMEM((128, 256), BF16),
            pltpu.VMEM((128, 128), F32),
            pltpu.VMEM((1, 64), BF16),
            pltpu.VMEM((64, 256), BF16),
            pltpu.VMEM((64, 256), BF16),
            pltpu.VMEM((64, 256), BF16),
            pltpu.VMEM((3, 64, 256), F32),
            pltpu.VMEM((2, 3, 16, 128), F32),
            pltpu.VMEM((2, 3, 16, 256), F32),
            pltpu.VMEM((2, 3, 16, 256), F32),
            pltpu.VMEM((4, 3, 16, 256), BF16),
            pltpu.SemaphoreType.DMA((len(SENT),)),
            pltpu.SemaphoreType.DMA((len(RECV),)),
            pltpu.SemaphoreType.DMA((6,)),
            pltpu.SemaphoreType.REGULAR((5,)),
        ],
        compiler_params=pltpu.CompilerParams(
            collective_id=0, has_side_effects=True, vmem_limit_bytes=60000000
        ),
    )(tokens, norm_gain.reshape(1, 64), gate_weight, up_weight, down_weight.T, slice_grads)


def solution(mesh):
    finer = Mesh(mesh.devices.reshape(mesh.shape["cuts"], 4, 4, 4, 2), CUTS_FSDP)
    in_specs = (
        P(CUTS_FSDP, None),
        P(FSDP),
        P(FSDP, None),
        P(FSDP, None),
        P(None, FSDP),
        P("cuts", None, FSDP, None),
    )
    out_specs = (P(CUTS_FSDP, None), P(None, FSDP, None))
    return jax.shard_map(
        per_device, mesh=finer, in_specs=in_specs, out_specs=out_specs, check_vma=False
    )
```

time: 63.5 us -> 56.2 us (0.89)
  Pallas kernels: 58.9 us -> 52.9 us
  local copies, waits for them, and re-layouts: 3.82 us -> 2 us
    pallas_call x1, Pallas kernels: 58.9 us -> 52.9 us  [per_device(): pl.pallas_call(kernel, out_shape=(pltpu.VMEM(tokens.shape, BF16), pltpu.V...]
    unnamed x4 -> x2, local copies, waits for them, and re-layouts: 3.82 us -> 2 us
where the time goes in v2:
time: 56.2 us; the launch traced here: 55.6 us
  Pallas kernels  52.9 us (94%)
  local copies, waits for them, and re-layouts  2 us (4%)
  between operations  0.64 us (1%)
    pallas_call x1, Pallas kernels, per_device(): pl.pallas_call(kernel, out_shape=(pltpu.VMEM(tokens.shape, BF16), pltpu.V...  52.9 us
    unnamed x2, local copies, waits for them, and re-layouts  2 us

profile of v2, /device:TPU:1, one launch (start us, length us, event | category | flops | bytes accessed | tf_op | source)
XLA Modules:
  0.0 55.6 jit_solution(107436556756398929)
XLA Ops:
  0.6 52.9 %shard_map.77 = (bf16[128,8192]{1,0:T(8,128)(2,1)S(1)}, f32[3,64,256]{2,1,0:T(8,128)S(1)}) custom-call(bf16[128,8192]{1,0:T(8,128)(2,1)} %tok_hbm.1, bf16[1,64]{1,0:T(2,128)(2,1)} %bitcast.3, bf16[64,256]{1,0:T(8,128)(2,1)} %gate_hbm.1, bf16[64,256]{1,0:T(8,128)(2,1)} %up_hbm.1, bf16[64,256]{1,0:T(8,128)(2,1)} %bitcast.2, f32[1,3,64,256]{3,2,1,0:T(8,128)} %grads_hbm.1), custom_call_target="tpu_custom_call" | custom-call | tf_op jit(solution)/shard_map/pallas_call | solution.py:520
  53.6 1.3 %copy.10 = bf16[128,8192]{1,0:T(8,128)(2,1)} copy(bf16[128,8192]{1,0:T(8,128)(2,1)S(1)} %get-tuple-element.2) | data formatting | bytes 4194304
  54.9 0.7 %copy.11 = f32[3,64,256]{2,1,0:T(8,128)} copy(f32[3,64,256]{2,1,0:T(8,128)S(1)} %get-tuple-element.3) | data formatting | bytes 393216

commit v3 on v2

--- a/solution.py
+++ b/solution.py
@@ -21,7 +21,8 @@
 RECV = [("t1", p, d) for p in PARTS for d in WAYS]
 RECV += [("t4", p) for p in PARTS] + [("z2", p) for p in PARTS] + [("c0", p) for p in PARTS]
 RECV += [("z1", p, d, j) for p in PARTS for d in WAYS for j in NEAR]
-RECV += [("g1", p, d, zr) for p in PARTS for d in WAYS for zr in NEAR]
+RECV += [("g1", p, d, zr) for p in PARTS for d in WAYS for zr in NEAR[1:]]
+RECV += [("g1", p, d, 0, j) for p in PARTS for d in WAYS for j in NEAR]
 RECV += [("g2", p, zr) for p in PARTS for zr in NEAR]
 RECV += [("d1", p, d, zr) for p in PARTS for d in WAYS for zr in NEAR[1:]]
 RECV += [("d2", p, zr) for p in PARTS for zr in NEAR[1:]]
@@ -197,7 +198,8 @@
 
     def along_last(p, zr, j):
         for e in WAYS:
-            give(("g1", p, e, zr), last[p], SIGN[e], p, j, zr, 0, rows=ALL if zr == 0 else GATED)
+            key = ("g1", p, e, zr, j) if zr == 0 else ("g1", p, e, zr)
+            give(key, last[p], SIGN[e], p, j, zr, 0, rows=ALL if zr == 0 else GATED)
 
     for p, d in BOTH:
         give(("t1", p, d), first[p], SIGN[d], p, 0, 0, 0)
@@ -250,30 +252,37 @@
     def _():
         four_away()
 
-    @pl.when(zg == 15)
-    def _():
-        told(1)
-        four_away()
-
-    @pl.when(zg < 13)
-    def _():
-        told(3)
-        exchange(0)
-
-    @pl.when(zg > 3)
-    def _():
-        told(4)
-        exchange(1)
-
     def first_axis(p, d):
         j = BACK[d]
         taken(("t1", p, d), p, j, 0, 0)
         give(("t4", p), first[p], SIGN[d], p, j, 0, 0, half=d)
-        along_z(p, j)
-        along_last(p, 0, j)
 
     for p, d in BOTH:
         first_axis(p, d)
+
+    @pl.when(zg == 15)
+    def _():
+        told(1)
+        four_away()
+
+    @pl.when(jnp.logical_and(zg > 7, zg < 13))
+    def _():
+        told(3)
+        exchange(0)
+
+    @pl.when(zg > 3)
+    def _():
+        told(4)
+        exchange(1)
+
+    for p, d in BOTH:
+        along_z(p, BACK[d])
+        along_last(p, 0, BACK[d])
+
+    @pl.when(zg < 8)
+    def _():
+        told(3)
+        exchange(0)
 
     def onward(p, d, j, half=True):
         give(("z2", p), "z", SIGN[d], p, j, BACK[d], 0, half=d if half else None)
@@ -317,12 +326,18 @@
     def gated_near(zr):
         for p, d in BOTH:
             r = BACK[d]
-            rows = ALL if zr == 0 else GATED
-            taken(("g1", p, d, zr), p, ALL, zr, r, rows=rows)
-            give(("g2", p, zr), last[p], SIGN[d], p, ALL, zr, r, half=d, rows=rows)
+            taken(("g1", p, d, zr), p, ALL, zr, r, rows=GATED)
+            give(("g2", p, zr), last[p], SIGN[d], p, ALL, zr, r, half=d, rows=GATED)
             give(("cg", p, r), "core", 1, p, ALL, zr, r, rows=GATED)
-            if zr == 0:
-                give(("cd", p, r), "core", 1, p, ALL, zr, r, rows=DOWN)
+
+    def own_near(j):
+        for p, d in BOTH:
+            r = BACK[d]
+            taken(("g1", p, d, 0, j), p, j, 0, r)
+            give(("g2", p, 0), last[p], SIGN[d], p, j, 0, r, half=d)
+            if j == 2:
+                give(("cg", p, r), "core", 1, p, ALL, 0, r, rows=GATED)
+                give(("cd", p, r), "core", 1, p, ALL, 0, r, rows=DOWN)
 
     def gated_far(zr):
         for p in PARTS:
@@ -365,17 +380,15 @@
                 total = total + jnp.dot(t, w, preferred_element_type=F32)
             acc[:, n] = total
 
-    def grads_partial():
-        for d in WAYS:
-            arrived(("rs1", d), rs1.at[d])
-            q = pl.ds(pl.multiple_of(ring(h, SIGN[d]) * 16, 16), 16)
-            part[d] = grad_in[:, q, :]
-            lanes = pl.ds(d * 128, 128)
-            part[d, :, :, lanes] = grad_in[:, q, lanes] + rs1[d]
-
-    def grads_send():
-        for d in WAYS:
-            copy_of(("rs2", d), part.at[d], rs2.at[d], "cut", SIGN[d]).start()
+    def grads_partial(d):
+        arrived(("rs1", d), rs1.at[d])
+        q = pl.ds(pl.multiple_of(ring(h, SIGN[d]) * 16, 16), 16)
+        part[d] = grad_in[:, q, :]
+        lanes = pl.ds(d * 128, 128)
+        part[d, :, :, lanes] = grad_in[:, q, lanes] + rs1[d]
+
+    def grads_send(d):
+        copy_of(("rs2", d), part.at[d], rs2.at[d], "cut", SIGN[d]).start()
 
     def grads_own():
         q = pl.ds(pl.multiple_of(h * 16, 16), 16)
@@ -393,9 +406,21 @@
             half = mean_out.at[ring(h, BACK[d]), :, :, pl.ds(d * 128, 128)]
             copy_of(("ag2", d), half, half, "cut", SIGN[d]).start()
 
+    own_near(0)
+
+    @pl.when(zg > 12)
+    def _():
+        told(3)
+        exchange(0)
+
     first_far(0)
     first_far(1)
-    from_z(1, (0,))
+    own_near(-1)
+    own_near(1)
+
+    @pl.when(zg < 15)
+    def _():
+        from_z(1, (0,))
 
     @pl.when(zg > 0)
     def _():
@@ -404,17 +429,44 @@
     @pl.when(zg == 0)
     def _():
         below()
+
+    @pl.when(zg < 2)
+    def _():
+        told(2)
+        four_away()
+
+    @pl.when(jnp.logical_and(zg < 4, zg != 1))
+    def _():
+        told(4)
+        exchange(1)
+
+    @pl.when(zg == 0)
+    def _():
         for p in PARTS:
             for j in NEAR:
                 give(("z1", p, 1, j), "z", -1, p, j, 0, 0)
             onward(p, 1, 0)
 
-    @pl.when(zg < 2)
-    def _():
-        told(2)
-        four_away()
-
-    gated_near(0)
+    own_near(2)
+
+    @pl.when(zg == 1)
+    def _():
+        told(4)
+        exchange(1)
+
+    @pl.when(zg > 11)
+    def _():
+        grads_partial(0)
+        grads_send(0)
+
+    @pl.when(zg == 15)
+    def _():
+        from_z(0, (-1, 1, 2))
+        down_near(-1)
+        grads_partial(1)
+        grads_send(1)
+        from_z(1, (0,))
+
     from_z(1, (-1, 1, 2))
 
     @pl.when(zg == 0)
@@ -425,35 +477,42 @@
 
     down_near(1)
 
-    @pl.when(zg > 12)
-    def _():
-        told(3)
-        exchange(0)
-
-    @pl.when(zg < 4)
-    def _():
-        told(4)
-        exchange(1)
-
-    grads_partial()
-    grads_send()
-
-    @pl.when(zg < 2)
+    @pl.when(jnp.logical_and(zg != 13, zg != 15))
+    def _():
+        grads_partial(1)
+        grads_send(1)
+
+    @pl.when(jnp.logical_or(zg == 0, jnp.logical_and(zg > 3, zg < 12)))
+    def _():
+        grads_partial(0)
+        grads_send(0)
+
+    @pl.when(zg == 0)
     def _():
         gated_near(1)
         down_next(1)
-
-    @pl.when(zg == 0)
-    def _():
         from_z(0, (0,))
 
-    from_z(0, (-1, 1, 2))
-    down_near(-1)
-
-    @pl.when(zg > 1)
+    @pl.when(zg < 15)
+    def _():
+        from_z(0, (-1, 1, 2))
+        down_near(-1)
+
+    @pl.when(zg == 13)
+    def _():
+        grads_partial(1)
+        grads_send(1)
+
+
+    @pl.when(zg > 0)
     def _():
         gated_near(1)
         down_next(1)
+
+    @pl.when(jnp.logical_and(zg > 0, zg < 4))
+    def _():
+        grads_partial(0)
+        grads_send(0)
 
     gated_near(-1)
     across_z()
@@ -462,7 +521,11 @@
     grads_own()
     grads_give()
     gated_near(2)
-    grads_next()
+
+    @pl.when(zg > 3)
+    def _():
+        grads_next()
+
     down_next(2)
     gated_far(0)
     gated_far(1)
@@ -508,6 +571,11 @@
             grad_out[:, k * 16 : k * 16 + 16, :] = mean_out[k].astype(F32)
 
     down_far(2)
+
+    @pl.when(zg < 4)
+    def _():
+        grads_next()
+
     lax.fori_loop(0, 3, near, 0)
     finish()
     last_part()

time: 56.2 us -> 51.8 us (0.922)
  the two profiles are of different devices: /device:TPU:1 before, /device:TPU:96 now
where the time goes in v3:
time: 51.8 us; the launch traced here: 51.7 us
  Pallas kernels  49 us (95%)
  local copies, waits for them, and re-layouts  2 us (4%)
  between operations  0.64 us (1%)
    pallas_call x1, Pallas kernels, per_device(): pl.pallas_call(kernel, out_shape=(pltpu.VMEM(tokens.shape, BF16), pltpu.V...  49 us
    unnamed x2, local copies, waits for them, and re-layouts  2 us

profile of v3, /device:TPU:96, one launch (start us, length us, event | category | flops | bytes accessed | tf_op | source)
XLA Modules:
  0.0 51.7 jit_solution(18537349350072750)
XLA Ops:
  0.6 49.0 %shard_map.77 = (bf16[128,8192]{1,0:T(8,128)(2,1)S(1)}, f32[3,64,256]{2,1,0:T(8,128)S(1)}) custom-call(bf16[128,8192]{1,0:T(8,128)(2,1)} %tok_hbm.1, bf16[1,64]{1,0:T(2,128)(2,1)} %bitcast.3, bf16[64,256]{1,0:T(8,128)(2,1)} %gate_hbm.1, bf16[64,256]{1,0:T(8,128)(2,1)} %up_hbm.1, bf16[64,256]{1,0:T(8,128)(2,1)} %bitcast.2, f32[1,3,64,256]{3,2,1,0:T(8,128)} %grads_hbm.1), custom_call_target="tpu_custom_call" | custom-call | tf_op jit(solution)/shard_map/pallas_call | solution.py:588
  49.7 1.3 %copy.10 = bf16[128,8192]{1,0:T(8,128)(2,1)} copy(bf16[128,8192]{1,0:T(8,128)(2,1)S(1)} %get-tuple-element.2) | data formatting | bytes 4194304
  51.0 0.7 %copy.11 = f32[3,64,256]{2,1,0:T(8,128)} copy(f32[3,64,256]{2,1,0:T(8,128)S(1)} %get-tuple-element.3) | data formatting | bytes 393216

commit v4 on v3

--- a/solution.py
+++ b/solution.py
@@ -35,10 +35,10 @@
 
 def kernel(
     tok_hbm, gain_hbm, gate_hbm, up_hbm, down_hbm, grads_hbm,
-    out, grad_out,
+    out, mean_out,
     buf_p, buf_q, tok, acc, hid, inv,
     gain_in, gate_in, up_in, down_in,
-    grad_in, rs1, part, rs2, mean_out,
+    grad_in, rs1, part, rs2,
     send_sem, recv_sem, in_sem, here,
 ):
     bufs = (buf_p, buf_q)
@@ -517,12 +517,16 @@
     gated_near(-1)
     across_z()
     down_near(2)
-    down_next(-1)
     grads_own()
     grads_give()
+    down_next(-1)
+    @pl.when(zg > 11)
+    def _():
+        grads_next()
+
     gated_near(2)
 
-    @pl.when(zg > 3)
+    @pl.when(jnp.logical_and(zg > 3, zg < 12))
     def _():
         grads_next()
 
@@ -567,8 +571,6 @@
     def finish():
         for d in WAYS:
             arrived(("ag2", d), mean_out.at[ring(h, 2), :, :, pl.ds(d * 128, 128)])
-        for k in range(4):
-            grad_out[:, k * 16 : k * 16 + 16, :] = mean_out[k].astype(F32)
 
     down_far(2)
 
@@ -577,19 +579,39 @@
         grads_next()
 
     lax.fori_loop(0, 3, near, 0)
+    last_part()
     finish()
-    last_part()
     all_sent()
+
+
+def write_out(branch, means, out_hbm, grad_hbm, grads, sems):
+    chunk = branch.shape[1] // 4
+    stores = [
+        pltpu.make_async_copy(
+            branch.at[:, k * chunk : (k + 1) * chunk],
+            out_hbm.at[:, k * chunk : (k + 1) * chunk],
+            sems.at[k],
+        )
+        for k in range(4)
+    ]
+    for store in stores:
+        store.start()
+    for k in range(4):
+        grads[:, k * 16 : k * 16 + 16, :] = means[k].astype(F32)
+    stores.append(pltpu.make_async_copy(grads, grad_hbm, sems.at[4]))
+    stores[4].start()
+    for store in stores:
+        store.wait()
 
 
 def per_device(tokens, norm_gain, gate_weight, up_weight, down_weight, slice_grads):
     hbm = pl.BlockSpec(memory_space=pltpu.HBM)
     vmem = pl.BlockSpec(memory_space=pltpu.VMEM)
-    return pl.pallas_call(
+    branch, means = pl.pallas_call(
         kernel,
         out_shape=(
             pltpu.VMEM(tokens.shape, BF16),
-            pltpu.VMEM(slice_grads.shape[1:], F32),
+            pltpu.VMEM((4, 3, 16, 256), BF16),
         ),
         in_specs=[hbm] * 6,
         out_specs=(vmem, vmem),
@@ -608,7 +630,6 @@
             pltpu.VMEM((2, 3, 16, 128), F32),
             pltpu.VMEM((2, 3, 16, 256), F32),
             pltpu.VMEM((2, 3, 16, 256), F32),
-            pltpu.VMEM((4, 3, 16, 256), BF16),
             pltpu.SemaphoreType.DMA((len(SENT),)),
             pltpu.SemaphoreType.DMA((len(RECV),)),
             pltpu.SemaphoreType.DMA((6,)),
@@ -618,6 +639,20 @@
             collective_id=0, has_side_effects=True, vmem_limit_bytes=60000000
         ),
     )(tokens, norm_gain.reshape(1, 64), gate_weight, up_weight, down_weight.T, slice_grads)
+    return pl.pallas_call(
+        write_out,
+        out_shape=(
+            pltpu.HBM(tokens.shape, BF16),
+            pltpu.HBM(slice_grads.shape[1:], F32),
+        ),
+        in_specs=[vmem, vmem],
+        out_specs=(hbm, hbm),
+        scratch_shapes=[
+            pltpu.VMEM(slice_grads.shape[1:], F32),
+            pltpu.SemaphoreType.DMA((5,)),
+        ],
+        compiler_params=pltpu.CompilerParams(vmem_limit_bytes=8 * 1024 * 1024),
+    )(branch, means)
 
 
 def solution(mesh):

time: 51.8 us -> 49.6 us (0.958)
  the two profiles are of different devices: /device:TPU:96 before, /device:TPU:1 now
where the time goes in v4:
time: 49.6 us; the launch traced here: 48.8 us
  Pallas kernels  48.2 us (97%)
  between operations  0.64 us (1%)
    pallas_call x1, Pallas kernels, per_device(): pl.pallas_call(kernel, out_shape=(pltpu.VMEM(tokens.shape, BF16), pltpu.V...  46.8 us
    pallas_call x1, Pallas kernels, per_device(): pl.pallas_call(write_out, out_shape=(pltpu.HBM(tokens.shape, BF16), pltpu...  1.41 us

profile of v4, /device:TPU:1, one launch (start us, length us, event | category | flops | bytes accessed | tf_op | source)
XLA Modules:
  0.0 48.8 jit_solution(15229159325855975423)
XLA Ops:
  0.6 46.8 %shard_map.77 = (bf16[128,8192]{1,0:T(8,128)(2,1)S(1)}, bf16[4,3,16,256]{3,2,1,0:T(8,128)(2,1)S(1)}) custom-call(bf16[128,8192]{1,0:T(8,128)(2,1)} %tok_hbm.1, bf16[1,64]{1,0:T(2,128)(2,1)} %bitcast.3, bf16[64,256]{1,0:T(8,128)(2,1)} %gate_hbm.1, bf16[64,256]{1,0:T(8,128)(2,1)} %up_hbm.1, bf16[64,256]{1,0:T(8,128)(2,1)} %bitcast.2, f32[1,3,64,256]{3,2,1,0:T(8,128)} %grads_hbm.1), custom_call_target="tpu_custom_call" | custom-call | tf_op jit(solution)/shard_map/pallas_call | solution.py:610
  47.4 1.4 %shard_map.78 = (bf16[128,8192]{1,0:T(8,128)(2,1)}, f32[3,64,256]{2,1,0:T(8,128)}) custom-call(bf16[128,8192]{1,0:T(8,128)(2,1)S(1)} %get-tuple-element.4.branch, bf16[4,3,16,256]{3,2,1,0:T(8,128)(2,1)S(1)} %get-tuple-element.5.means), custom_call_target="tpu_custom_call" | custom-call | tf_op jit(solution)/shard_map/pallas_call | solution.py:642

commit v5 on v4

--- a/solution.py
+++ b/solution.py
@@ -533,11 +533,25 @@
     down_next(2)
     gated_far(0)
     gated_far(1)
+
+    @pl.when(c == 1)
+    def _():
+        gated_far(-1)
+        gated_far(2)
+
     multiply(0)
-    gated_far(-1)
+
+    @pl.when(c == 0)
+    def _():
+        gated_far(-1)
+
     multiply(-1)
-    gated_far(2)
     multiply(1)
+
+    @pl.when(c == 0)
+    def _():
+        gated_far(2)
+
     down_far(1)
     down_far(-1)
     multiply(2)
@@ -578,7 +592,8 @@
     def _():
         grads_next()
 
-    lax.fori_loop(0, 3, near, 0)
+    for k in range(3):
+        near(k, 0)
     last_part()
     finish()
     all_sent()
@@ -594,8 +609,8 @@
         )
         for k in range(4)
     ]
-    for store in stores:
-        store.start()
+    for k, store in enumerate(stores):
+        store.start(priority=k % 2)
     for k in range(4):
         grads[:, k * 16 : k * 16 + 16, :] = means[k].astype(F32)
     stores.append(pltpu.make_async_copy(grads, grad_hbm, sems.at[4]))

time: 49.6 us -> 49.6 us (level)
  no operation moved by 1% of the time
where the time goes in v5:
time: 49.6 us; the launch traced here: 48.7 us
  Pallas kernels  48.1 us (97%)
  between operations  0.64 us (1%)
    pallas_call x1, Pallas kernels, per_device(): pl.pallas_call(kernel, out_shape=(pltpu.VMEM(tokens.shape, BF16), pltpu.V...  46.6 us
    pallas_call x1, Pallas kernels, per_device(): pl.pallas_call(write_out, out_shape=(pltpu.HBM(tokens.shape, BF16), pltpu...  1.42 us

profile of v5, /device:TPU:1, one launch (start us, length us, event | category | flops | bytes accessed | tf_op | source)
XLA Modules:
  0.0 48.7 jit_solution(10823333034701889405)
XLA Ops:
  0.6 46.6 %shard_map.77 = (bf16[128,8192]{1,0:T(8,128)(2,1)S(1)}, bf16[4,3,16,256]{3,2,1,0:T(8,128)(2,1)S(1)}) custom-call(bf16[128,8192]{1,0:T(8,128)(2,1)} %tok_hbm.1, bf16[1,64]{1,0:T(2,128)(2,1)} %bitcast.3, bf16[64,256]{1,0:T(8,128)(2,1)} %gate_hbm.1, bf16[64,256]{1,0:T(8,128)(2,1)} %up_hbm.1, bf16[64,256]{1,0:T(8,128)(2,1)} %bitcast.2, f32[1,3,64,256]{3,2,1,0:T(8,128)} %grads_hbm.1), custom_call_target="tpu_custom_call" | custom-call | tf_op jit(solution)/shard_map/pallas_call | solution.py:625
  47.3 1.4 %shard_map.78 = (bf16[128,8192]{1,0:T(8,128)(2,1)}, f32[3,64,256]{2,1,0:T(8,128)}) custom-call(bf16[128,8192]{1,0:T(8,128)(2,1)S(1)} %get-tuple-element.4.branch, bf16[4,3,16,256]{3,2,1,0:T(8,128)(2,1)S(1)} %get-tuple-element.5.means), custom_call_target="tpu_custom_call" | custom-call | tf_op jit(solution)/shard_map/pallas_call | solution.py:657
